TPU v7x, 32 devices: a whole 2x2x4 slice. The times are simulated.
32 devices in a mesh: groups: 2 (over y), seq: 4 (over z), head: 2 (over x), rep: 2 (over core).
Axes of the slice: x: 2, y: 2, z: 4, core: 2. Of those that a mesh axis runs over, the one named last changes fastest.
Arguments:
- queries: bfloat16 [2048, 6144], P(('groups', 'seq', 'rep'), 'head'), parts along dimension 0, may hold values from -150 to 150
- key_tokens: bfloat16 [2048, 6144], P(('groups', 'seq', 'rep'), 'head'), parts along dimension 0, may hold values from -6 to 6
- value_tokens: bfloat16 [2048, 6144], P(('groups', 'seq', 'rep'), 'head'), parts along dimension 0, may hold values from -6 to 6
- stream: bfloat16 [2048, 6144], P(('groups', 'seq', 'rep'), 'head'), parts along dimension 0, may hold values from -6 to 6
- norm_gain: float32 [6144], P('head'), may hold values from 0.1 to 1.9
- latent_weight: bfloat16 [6144, 64], P('head'), may hold values from -0.078125 to 0.078125
- tile_pool: bfloat16 [8, 64, 2, 128], P(('groups', 'seq')), parts along dimension 0, may hold values from -6 to 6
- tile_position: int32 [8], P('groups'), parts along dimension 0, may hold values from 0 to 3, each once
- lift_weight: bfloat16 [64, 512], P(None, ('head', 'rep')), may hold values from -0.75 to 0.75
- lift_bias: float32 [512], P(('head', 'rep')), may hold values from -3 to 3
- conv_weight: bfloat16 [2, 27, 512, 512], P(None, None, ('head', 'rep')), may hold values from -0.0546875 to 0.0546875
Outputs:
- hidden: bfloat16 [2048, 6144], P(('groups', 'seq', 'rep'), 'head'), parts along dimension 0
- latents: float32 [2048, 64], P(('groups', 'seq', 'rep')), parts along dimension 0
- decoded: float32 [1024, 2, 4, 128], P(('groups', 'head', 'rep'), None, 'seq'), parts along dimension 0
There are 2 independent parts, one for each index of `groups`. A program takes and returns all parts, laid end to end along the dimension named above; an argument that names none is the same for every part. Nothing has to cross between parts.
Inputs may be any that keep to these rules, and one draw needn't show every extreme that they name: `tile_position`: each of the 4 grid rows is named by exactly one pool tile.
All inputs are finite; a program needn't handle non-finite values.
Results may differ from a plain program's by a relative error of at most 0.01.
Values may be sent and summed in bfloat16 or wider, within the bound.
A program may use at most 128 MiB of HBM per device.

v0:
```python
import functools
import math

import jax
import jax.numpy as jnp
from jax import lax
from jax.experimental import pallas as pl
from jax.experimental.pallas import tpu as pltpu
from jax.sharding import PartitionSpec as P

HEAD_DIM = 128
WIDTH = 6144


epsilon = 1e-06
negative = -1e30


def padded(shard, sides, width):
    for axis, dim in sides:
        peers, length = (lax.axis_size(axis), shard.shape[dim])
        up = [(i, (i + 1) % peers) for i in range(peers - 1)]
        down = [(j, i) for i, j in up]
        last = lax.slice_in_dim(shard, length - width, length, axis=dim)
        leading = lax.slice_in_dim(shard, 0, width, axis=dim)
        before = lax.ppermute(last, axis, up)
        after = lax.ppermute(leading, axis, down)
        shard = jnp.concatenate([before, shard, after], axis=dim)
    return shard


def prepare(block_rows):
    row_count = block_rows.shape[0]
    head_count = block_rows.shape[1] // HEAD_DIM
    query_heads = block_rows.reshape(row_count, head_count, HEAD_DIM)
    initial = (
        jnp.full((head_count, row_count), negative, jnp.float32),
        jnp.zeros((head_count, row_count), jnp.float32),
        jnp.zeros((head_count, row_count, HEAD_DIM), jnp.float32),
    )
    return (query_heads, initial)


def make_update(query_heads, state, pieces):
    head_count = query_heads.shape[1]
    factor = 1.0 / math.sqrt(HEAD_DIM)
    running_max, running_sum, accum = state
    key_piece, value_piece = pieces
    piece_rows = key_piece.shape[0]
    key_heads = key_piece.reshape(piece_rows, head_count, HEAD_DIM)
    value_heads = value_piece.reshape(piece_rows, head_count, HEAD_DIM)
    scores = (
        jnp.einsum("qhd,khd->hqk", query_heads, key_heads, preferred_element_type=jnp.float32)
        * factor
    )
    new_max = jnp.maximum(running_max, jnp.max(scores, axis=2))
    exponent = jnp.exp(scores - new_max[:, :, None])
    running_sum = jnp.sum(exponent, axis=2)
    accum = jnp.einsum(
        "hqk,khd->hqd",
        exponent.astype(jnp.bfloat16),
        value_heads,
        preferred_element_type=jnp.float32,
    )
    return (new_max, running_sum, accum)


def finish(state):
    running_max, running_sum, accum = state
    result = accum / running_sum[:, :, None]
    return jnp.transpose(result, (1, 0, 2)).reshape(result.shape[1], -1).astype(jnp.bfloat16)


def shift_columns(window, col_shift):
    if col_shift == 0:
        return window
    edge = jnp.zeros(window.shape[:-1] + (1,), window.dtype)
    if col_shift < 0:
        return jnp.concatenate([edge, window[..., :-1]], axis=-1)
    return jnp.concatenate([window[..., 1:], edge], axis=-1)


def tap_sum(running, piece_block, layer_weight):
    piece_rows = piece_block.shape[0]
    frames = piece_block.shape[1]
    band_rows = piece_block.shape[2] - 2
    framed = jnp.pad(piece_block, ((0, 0), (1, 1), (0, 0), (0, 0)))
    for frame_off in range(3):
        for row_off in range(3):
            for col_off in range(3):
                window = shift_columns(
                    framed[:, frame_off : frame_off + frames, row_off : row_off + band_rows, :],
                    col_off - 1,
                )
                tap_weight = layer_weight[frame_off * 9 + row_off * 3 + col_off]
                running = running + lax.dot_general(
                    tap_weight,
                    window.reshape(piece_rows, -1),
                    (((1,), (0,)), ((), ())),
                    preferred_element_type=jnp.float32,
                )
    return running


def make_pick(tile_position, own_rows, piece_block):
    selector = (own_rows[:, None] == tile_position[None, :]).astype(jnp.bfloat16)
    return jnp.einsum("tp,plfc->lftc", selector, piece_block, preferred_element_type=jnp.float32)


MESH = pl.DeviceIdType.MESH


def fused_kernel(
    seq_size, rep_size, head_size,
    q_hbm, k_hbm, v_hbm, stream_hbm, gain_ref, lw_ref,
    tile_ref, place_ref, lift_ref, bias_ref, conv_ref,
    hid_hbm, sums_ref, dec_ref,
    q_ref, k_ref, v_ref, stream_ref, hid_ref,
    qkv, obuf, att, part, part_in,
    tiles, lifts, biases, taps, act1, act2, feat, acc,
    send_sem, recv_sem, osend_sem, orecv_sem, psend_sem, precv_sem,
    load_sem, hid_sem, tap_sem, dsend_sem, drecv_sem,
):
    loads = [
        pltpu.make_async_copy(source, target, load_sem.at[i])
        for i, (source, target) in enumerate(
            ((q_hbm, q_ref), (k_hbm, k_ref), (v_hbm, v_ref), (stream_hbm, stream_ref))
        )
    ]
    for load in loads:
        load.start()
    seq, rep, head = (lax.axis_index(a) for a in ("seq", "rep", "head"))
    count = seq_size * rep_size
    me = seq * rep_size + rep
    rows = q_ref.shape[0]
    own_heads = qkv.shape[0]
    others = count - 1
    factor = 1.0 / math.sqrt(HEAD_DIM)
    offsets = [(d, e) for d in (2, 1, 3, 0) for e in range(rep_size) if (d, e) != (0, 0)]

    def peer(d, e):
        return lax.rem(seq + d, seq_size), lax.rem(rep + e, rep_size)

    partner = {"head": lax.rem(head + 1, head_size)}
    mates = [
        {"head": lax.rem(head + d, head_size), "rep": lax.rem(rep + e, rep_size)}
        for d in range(head_size) for e in range(rep_size) if (d, e) != (0, 0)
    ]
    quarter = head * rep_size + rep
    tap_copy = pltpu.make_async_copy(conv_ref, taps, tap_sem)
    tap_copy.start()
    barrier = pltpu.get_barrier_semaphore()
    for d, e in offsets:
        ps, pr = peer(d, e)
        pl.semaphore_signal(barrier, inc=1, device_id={"seq": ps, "rep": pr}, device_id_type=MESH)
    strangers = [m for m, e in zip(mates, range(1, head_size * rep_size)) if e >= rep_size]
    for mate in strangers:
        pl.semaphore_signal(barrier, inc=1, device_id=mate, device_id_type=MESH)
    pl.semaphore_wait(barrier, others + len(strangers))

    def arrived(ref, sem):
        pltpu.make_async_copy(ref, ref, sem).wait()

    def send(source, target, index, device):
        pltpu.make_async_remote_copy(
            src_ref=source, dst_ref=target,
            send_sem=dsend_sem.at[index], recv_sem=drecv_sem.at[index],
            device_id=device, device_id_type=MESH,
        ).start()

    share = tile_ref.shape[1] // (head_size * rep_size)
    my_share = pl.ds(pl.multiple_of(quarter * share, share), share)
    for d in range(1, seq_size):
        send(tile_ref.at[0, my_share], tiles.at[seq, my_share], 0,
             {"seq": lax.rem(seq + d, seq_size)})
    for mate in mates:
        send(lift_ref, lifts.at[quarter], 1, mate)
        send(bias_ref, biases.at[quarter], 2, mate)

    for load in loads[:3]:
        load.wait()
    my_rows = pl.ds(pl.multiple_of(me * rows, rows), rows)
    sources = (q_ref, k_ref, v_ref)
    for h in range(own_heads):
        for d, e in offsets:
            ps, pr = peer(d, e)
            column = ((ps * rep_size + pr) * own_heads + h) * HEAD_DIM
            columns = pl.ds(pl.multiple_of(column, HEAD_DIM), HEAD_DIM)
            for a, source in enumerate(sources):
                pltpu.make_async_remote_copy(
                    src_ref=source.at[:, columns],
                    dst_ref=qkv.at[h, a, my_rows, :],
                    send_sem=send_sem,
                    recv_sem=recv_sem.at[h],
                    device_id={"seq": ps, "rep": pr},
                    device_id_type=MESH,
                ).start()
    for h in range(own_heads):
        columns = pl.ds(pl.multiple_of((me * own_heads + h) * HEAD_DIM, HEAD_DIM), HEAD_DIM)
        for a, source in enumerate(sources):
            qkv[h, a, my_rows, :] = source[:, columns]

    tiles[seq, my_share] = tile_ref[0, my_share]
    lifts[quarter] = lift_ref[...]
    biases[quarter] = bias_ref[...]
    pieces = len(mates)
    arrived(tiles.at[pl.ds(0, seq_size - 1), pl.ds(0, share)], drecv_sem.at[0])
    for mate in mates:
        send(tiles.at[:, my_share], tiles.at[:, my_share], 3, mate)
    arrived(lifts.at[pl.ds(0, pieces)], drecv_sem.at[1])
    arrived(biases.at[pl.ds(0, pieces)], drecv_sem.at[2])
    arrived(tiles.at[:, pl.ds(0, pieces * share)], drecv_sem.at[3])

    frames, reach, columns_here, channels = act1.shape
    own = lift_ref.shape[1]
    margin = reach // 2
    own_lanes = pl.ds(pl.multiple_of(quarter * own, own), own)

    def inside(d):
        row = seq + d
        return jnp.where(jnp.logical_and(row >= 0, row < seq_size), 1.0, 0.0)

    def silu(value):
        return value / (1.0 + jnp.exp(-value))

    def lifted(chosen, weight, bias):
        return lax.dot_general(
            chosen, weight, (((0,), (0,)), ((), ())), preferred_element_type=jnp.float32
        ) + bias

    wide = [tiles[p].astype(jnp.float32) for p in range(seq_size)]
    for d in range(reach):
        picked = jnp.zeros(wide[0].shape, jnp.float32)
        for p in range(seq_size):
            picked = picked + jnp.where(place_ref[p] == seq + d - margin, 1.0, 0.0) * wide[p]
        for f in range(frames):
            chosen = picked[:, f, :].astype(jnp.bfloat16)
            for c in range(pieces + 1):
                active = silu(lifted(chosen, lifts[c], biases[c])) * inside(d - margin)
                act1[f, d, :, c * own:(c + 1) * own] = active.astype(jnp.bfloat16)
            if 1 <= d <= reach - 2:
                feat[f, d - 1] = lifted(chosen, lift_ref[...], bias_ref[...])

    def convolve(layer, active, rows_out):
        length = rows_out * columns_here
        for f in range(frames):
            first = True
            for a in range(3):
                if not 0 <= f + a - 1 < frames:
                    continue
                for b in range(3):
                    window = active[f + a - 1, b:b + rows_out].reshape(length, channels)
                    base = 9 * a + 3 * b
                    term = lax.dot_general(
                        window, taps[layer, base:base + 3].reshape(3 * own, channels),
                        (((1,), (1,)), ((), ())), preferred_element_type=jnp.float32,
                    )
                    acc[f, :length, :] = term if first else acc[f, :length, :] + term
                    first = False

    def gathered_columns(f, r):
        lines = slice(r * columns_here, (r + 1) * columns_here)
        at = lax.broadcasted_iota(jnp.int32, (columns_here, own), 0)
        before = pltpu.roll(acc[f, lines, :own], 1, 0)
        after = pltpu.roll(acc[f, lines, 2 * own:], columns_here - 1, 0)
        return (
            acc[f, lines, own:2 * own]
            + jnp.where(at == 0, 0.0, before)
            + jnp.where(at == columns_here - 1, 0.0, after)
        )

    tap_copy.wait()
    convolve(0, act1, reach - 2)
    for f in range(frames):
        for r in range(reach - 2):
            value = feat[f, r] + gathered_columns(f, r)
            feat[f, r] = value
            act2[f, r, :, own_lanes] = (silu(value) * inside(r + 1 - margin)).astype(jnp.bfloat16)
    for mate in mates:
        send(act2.at[:, :, :, own_lanes], act2.at[:, :, :, own_lanes], 4, mate)

    def last_layer():
        arrived(act2.at[:, :, :, pl.ds(0, pieces * own)], drecv_sem.at[4])
        convolve(1, act2, reach - 4)
        for f in range(frames):
            dec_ref[f * columns_here:(f + 1) * columns_here, :] = (
                feat[f, margin - 1] + gathered_columns(f, 0)
            )

    block = rep_size * rows
    for h in range(own_heads):
        arrived(qkv.at[h, :, pl.ds(0, others * rows), :], recv_sem.at[h])
        out_columns = pl.ds(pl.multiple_of((me * own_heads + h) * HEAD_DIM, HEAD_DIM), HEAD_DIM)

        def attend(step, carry):
            target = lax.rem(seq + 2 + step, seq_size)
            here = pl.ds(pl.multiple_of(target * block, block), block)
            scores = lax.dot_general(
                qkv[h, 0, here, :], qkv[h, 1], (((1,), (1,)), ((), ())),
                preferred_element_type=jnp.float32,
            ) * factor
            exponent = jnp.exp(scores - jnp.max(scores, axis=1, keepdims=True))
            total = jnp.sum(exponent, axis=1, keepdims=True)
            summed = jnp.dot(
                exponent.astype(jnp.bfloat16), qkv[h, 2], preferred_element_type=jnp.float32
            )
            obuf[h, here, :] = (summed / total).astype(jnp.bfloat16)
            for r in range(rep_size):
                @pl.when(jnp.logical_or(target != seq, rep != r))
                def _():
                    start = pl.multiple_of(target * block + r * rows, rows)
                    pltpu.make_async_remote_copy(
                        src_ref=obuf.at[h, pl.ds(start, rows), :],
                        dst_ref=att.at[:, out_columns],
                        send_sem=osend_sem,
                        recv_sem=orecv_sem.at[h],
                        device_id={"seq": target, "rep": r},
                        device_id_type=MESH,
                    ).start()
            return carry

        lax.fori_loop(0, seq_size, attend, 0)
        att[:, out_columns] = obuf[h, my_rows, :]
        if h == own_heads - 1:
            last_layer()

    loads[3].wait()
    squares = jnp.zeros((rows, HEAD_DIM), jnp.float32)
    projected = jnp.zeros((rows, lw_ref.shape[0]), jnp.float32)
    for h in range(own_heads):
        arrived(obuf.at[h, pl.ds(0, others * rows), :], orecv_sem.at[h])
        for j in range(count):
            low = (j * own_heads + h) * HEAD_DIM
            cols = slice(low, low + HEAD_DIM)
            combined = stream_ref[:, cols].astype(jnp.float32) + att[:, cols].astype(jnp.float32)
            hidden = combined.astype(jnp.bfloat16)
            hid_ref[:, cols] = hidden
            widened = hidden.astype(jnp.float32)
            squares = squares + widened * widened
            scaled = (widened * gain_ref[:, cols]).astype(jnp.bfloat16)
            projected = projected + lax.dot_general(
                scaled, lw_ref[:, cols], (((1,), (1,)), ((), ())),
                preferred_element_type=jnp.float32,
            )
    latent = projected.shape[1]
    summed = jnp.sum(squares, axis=1, keepdims=True)
    part[:, :latent] = projected
    part[:, latent:] = jnp.broadcast_to(summed, (rows, part.shape[1] - latent))
    swap = pltpu.make_async_remote_copy(
        src_ref=part, dst_ref=part_in, send_sem=psend_sem, recv_sem=precv_sem,
        device_id=partner, device_id_type=MESH,
    )
    swap.start()
    hid_copy = pltpu.make_async_copy(hid_ref, hid_hbm, hid_sem)
    hid_copy.start()
    arrived(qkv.at[:, :, pl.ds(0, others * rows), :], send_sem)
    arrived(obuf.at[:, pl.ds(0, others * rows), :], osend_sem)
    swap.wait()
    arrived(tiles.at[pl.ds(0, seq_size - 1), pl.ds(0, share)], dsend_sem.at[0])
    arrived(lifts.at[pl.ds(0, pieces)], dsend_sem.at[1])
    arrived(biases.at[pl.ds(0, pieces)], dsend_sem.at[2])
    arrived(tiles.at[:, pl.ds(0, pieces * share)], dsend_sem.at[3])
    arrived(act2.at[:, :, :, pl.ds(0, pieces * own)], dsend_sem.at[4])
    sums_ref[...] = part[...] + part_in[...]
    hid_copy.wait()


def finish_kernel(
    full_width, hid_in, sums_ref, dec_in, hid_out, lat_ref, dec_ref, held, in_sem, out_sem
):
    chunks = held.shape[0]
    size = hid_in.shape[0] // chunks
    reads = [
        pltpu.make_async_copy(hid_in.at[pl.ds(i * size, size), :], held.at[i], in_sem.at[i])
        for i in range(chunks)
    ]
    writes = [
        pltpu.make_async_copy(held.at[i], hid_out.at[pl.ds(i * size, size), :], out_sem.at[i])
        for i in range(chunks)
    ]
    for read in reads:
        read.start()
    for read, write in zip(reads, writes):
        read.wait()
        write.start()
    latent = lat_ref.shape[0]
    sums = jnp.transpose(sums_ref[...])
    lat_ref[...] = sums[:latent] * lax.rsqrt(sums[latent:latent + 1] / full_width + epsilon)
    frames = dec_ref.shape[0] // dec_in.shape[1]
    columns = dec_in.shape[0] // frames
    for f in range(frames):
        dec_ref[pl.ds(f, dec_in.shape[1], stride=frames), :] = jnp.transpose(
            dec_in[f * columns:(f + 1) * columns, :]
        )
    for write in writes:
        write.wait()


def fused(
    queries, key_tokens, value_tokens, stream, norm_gain, latent_weight,
    tile_pool, tile_position, lift_weight, lift_bias, conv_weight,
):
    seq_size, rep_size, head_size = (lax.axis_size(a) for a in ("seq", "rep", "head"))
    rows, width = queries.shape
    count = seq_size * rep_size
    own_heads = width // HEAD_DIM // count
    latent = latent_weight.shape[1]
    lanes = 2 * latent
    depth, frames, columns = tile_pool.shape[1:]
    layers, _, own, channels = conv_weight.shape
    quarters = head_size * rep_size
    reach = 2 * layers + 1
    bf = jnp.bfloat16
    vmem = pl.BlockSpec(memory_space=pltpu.VMEM)
    hbm = pl.BlockSpec(memory_space=pltpu.HBM)
    smem = pl.BlockSpec(memory_space=pltpu.SMEM)
    dma = pltpu.SemaphoreType.DMA
    hidden, sums, decoded = pl.pallas_call(
        functools.partial(fused_kernel, seq_size, rep_size, head_size),
        out_shape=(
            jax.ShapeDtypeStruct((rows, width), bf),
            jax.ShapeDtypeStruct((rows, lanes), jnp.float32),
            jax.ShapeDtypeStruct((frames * columns, own), jnp.float32),
        ),
        in_specs=[hbm] * 4 + [vmem] * 3 + [smem, vmem, vmem, hbm],
        out_specs=(hbm, vmem, vmem),
        scratch_shapes=[pltpu.VMEM((rows, width), bf)] * 5 + [
            pltpu.VMEM((own_heads, 3, count * rows, HEAD_DIM), bf),
            pltpu.VMEM((own_heads, count * rows, HEAD_DIM), bf),
            pltpu.VMEM((rows, width), bf),
            pltpu.VMEM((rows, lanes), jnp.float32),
            pltpu.VMEM((rows, lanes), jnp.float32),
            pltpu.VMEM((seq_size, depth, frames, columns), bf),
            pltpu.VMEM((quarters, depth, own), bf),
            pltpu.VMEM((quarters, 1, own), jnp.float32),
            pltpu.VMEM(conv_weight.shape, bf),
            pltpu.VMEM((frames, reach, columns, channels), bf),
            pltpu.VMEM((frames, reach - 2, columns, channels), bf),
            pltpu.VMEM((frames, reach - 2, columns, own), jnp.float32),
            pltpu.VMEM((frames, (reach - 2) * columns, 3 * own), jnp.float32),
            dma, dma((own_heads,)), dma, dma((own_heads,)), dma, dma,
            dma((4,)), dma, dma, dma((5,)), dma((5,)),
        ],
        compiler_params=pltpu.CompilerParams(
            collective_id=0, has_side_effects=True, vmem_limit_bytes=56 << 20
        ),
    )(
        queries, key_tokens, value_tokens, stream, norm_gain[None, :], latent_weight.T,
        tile_pool, tile_position, lift_weight, lift_bias[None, :], conv_weight,
    )
    chunks = 4
    hidden, latents, decoded = pl.pallas_call(
        functools.partial(finish_kernel, width * head_size),
        out_shape=(
            jax.ShapeDtypeStruct((rows, width), bf),
            jax.ShapeDtypeStruct((latent, rows), jnp.float32),
            jax.ShapeDtypeStruct((own * frames, columns), jnp.float32),
        ),
        in_specs=[hbm, vmem, vmem],
        out_specs=(hbm, vmem, vmem),
        scratch_shapes=[
            pltpu.VMEM((chunks, rows // chunks, width), bf), dma((chunks,)), dma((chunks,)),
        ],
    )(hidden, sums, decoded)
    return hidden, latents.T, decoded.reshape(own, frames, 1, columns)


def gathered(queries, key_tokens, value_tokens, stream, norm_gain, latent_weight):
    query_heads, initial = prepare(queries)
    state = make_update(
        query_heads,
        initial,
        (
            lax.all_gather(key_tokens, ("seq", "rep"), axis=0, tiled=True),
            lax.all_gather(value_tokens, ("seq", "rep"), axis=0, tiled=True),
        ),
    )
    attended = finish(state)
    combined = stream.astype(jnp.float32) + attended.astype(jnp.float32)
    hidden = combined.astype(jnp.bfloat16)
    widened = hidden.astype(jnp.float32)
    scaled = (widened * norm_gain).astype(jnp.bfloat16)
    partial_proj = jnp.dot(scaled, latent_weight, preferred_element_type=jnp.float32)
    partial_squares = jnp.sum(widened * widened, axis=1)
    projected, squares = (
        lax.psum(partial_proj.astype(jnp.bfloat16), "head").astype(jnp.float32),
        lax.psum(partial_squares.astype(jnp.bfloat16), "head").astype(jnp.float32),
    )
    latents = projected * lax.rsqrt(squares / WIDTH + epsilon)[:, None]
    return hidden, latents


def shards(
    queries,
    key_tokens,
    value_tokens,
    stream,
    norm_gain,
    latent_weight,
    tile_pool,
    tile_position,
    lift_weight,
    lift_bias,
    conv_weight,
):
    heads_here = queries.shape[1] // HEAD_DIM
    spread = lax.axis_size("seq") * lax.axis_size("rep")
    fits = heads_here % spread == 0 and lax.axis_size("seq") == 4 and lax.axis_size("head") == 2
    fits = fits and lax.axis_size("rep") == 2 and tile_pool.shape[0] == 1
    fits = fits and conv_weight.shape[0] == 2 and lift_weight.shape[0] % 64 == 0
    if fits:
        return fused(
            queries, key_tokens, value_tokens, stream, norm_gain, latent_weight,
            tile_pool, tile_position, lift_weight, lift_bias, conv_weight,
        )
    hidden, latents = gathered(
        queries, key_tokens, value_tokens, stream, norm_gain, latent_weight
    )
    tiles_here = tile_pool.shape[0]
    frames = tile_pool.shape[2]
    columns = tile_pool.shape[3]
    own_rows = lax.axis_index("seq") * tiles_here + jnp.arange(tiles_here, dtype=jnp.int32)
    collected = make_pick(
        tile_position, own_rows, lax.all_gather(tile_pool, "seq", axis=0, tiled=True)
    )
    latent_grid = collected.astype(jnp.bfloat16)
    channels_here = lift_weight.shape[1]
    feature_map = (
        lax.dot_general(
            lift_weight,
            latent_grid.reshape(latent_grid.shape[0], -1),
            (((0,), (0,)), ((), ())),
            preferred_element_type=jnp.float32,
        )
        + lift_bias[:, None]
    )
    for layer_index in range(conv_weight.shape[0]):
        layer_weight = conv_weight[layer_index]
        active = (
            jax.nn.silu(feature_map)
            .astype(jnp.bfloat16)
            .reshape(channels_here, frames, tiles_here, columns)
        )
        zeros_here = jnp.zeros(feature_map.shape, jnp.float32)
        bordered = padded(active, (("seq", 2),), 1)
        rimmed = lax.all_gather(bordered, ("head", "rep"), axis=0, tiled=True)
        update = tap_sum(zeros_here, rimmed, layer_weight)
        feature_map = feature_map + update
    decoded = feature_map.reshape(channels_here, frames, tiles_here, columns)
    return (hidden, latents, decoded)


def solution(mesh):
    in_specs = (
        P(("groups", "seq", "rep"), "head"),
        P(("groups", "seq", "rep"), "head"),
        P(("groups", "seq", "rep"), "head"),
        P(("groups", "seq", "rep"), "head"),
        P("head"),
        P("head", None),
        P(("groups", "seq"), None, None, None),
        P("groups"),
        P(None, ("head", "rep")),
        P(("head", "rep")),
        P(None, None, ("head", "rep"), None),
    )
    out_specs = (
        P(("groups", "seq", "rep"), "head"),
        P(("groups", "seq", "rep"), None),
        P(("groups", "head", "rep"), None, "seq", None),
    )
    return jax.shard_map(shards, mesh=mesh, in_specs=in_specs, out_specs=out_specs, check_vma=False)
```

profile of v0, /device:TPU:0, one launch (start us, length us, event | category | flops | bytes accessed | tf_op | source)
XLA Modules:
  0.0 83.9 jit_solution(10263709028540336745)
XLA Ops:
  0.6 79.7 %shard_map.130 = (bf16[128,3072]{1,0:T(8,128)(2,1)}, f32[128,128]{1,0:T(8,128)}, f32[256,128]{1,0:T(8,128)}) custom-call(bf16[128,3072]{1,0:T(8,128)(2,1)} %q_hbm.1, bf16[128,3072]{1,0:T(8,128)(2,1)} %k_hbm.1, bf16[128,3072]{1,0:T(8,128)(2,1)} %v_hbm.1, bf16[128,3072]{1,0:T(8,128)(2,1)} %stream_hbm.1, f32[1,3072]{1,0:T(1,128)} %bitcast.8, ...), custom_call_target="tpu_custom_call" | custom-call | tf_op jit(solution)/shard_map/pallas_call | solution.py:418
  80.3 3.6 %shard_map.131 = (bf16[128,3072]{1,0:T(8,128)(2,1)}, f32[64,128]{1,0:T(8,128)}, f32[256,128]{1,0:T(8,128)}) custom-call(bf16[128,3072]{1,0:T(8,128)(2,1)} %get-tuple-element.9.hid_in, f32[128,128]{1,0:T(8,128)} %get-tuple-element.10.sums_ref, f32[256,128]{1,0:T(8,128)} %get-tuple-element.11.dec_in), custom_call_target="tpu_custom_call" | custom-call | tf_op jit(solution)/shard_map/pallas_call | solution.py:452
where the time goes:
time: 84.1 us; the launch traced here: 83.9 us
  Pallas kernels  83.2 us (99%)
    pallas_call x1, Pallas kernels, fused(): pl.pallas_call(functools.partial(fused_kernel, seq_size, rep_size, head_s...  79.7 us
    pallas_call x1, Pallas kernels, fused(): pl.pallas_call(functools.partial(finish_kernel, width * head_size), out_s...  3.57 us

commit v1 on v0

--- a/solution.py
+++ b/solution.py
@@ -111,24 +111,17 @@
 
 
 def fused_kernel(
-    seq_size, rep_size, head_size,
-    q_hbm, k_hbm, v_hbm, stream_hbm, gain_ref, lw_ref,
-    tile_ref, place_ref, lift_ref, bias_ref, conv_ref,
-    hid_hbm, sums_ref, dec_ref,
-    q_ref, k_ref, v_ref, stream_ref, hid_ref,
+    seq_size, rep_size, head_size, full_width,
+    q_hbm, k_hbm, v_hbm, stream_hbm, gain_hbm, lw_hbm,
+    tile_hbm, place_hbm, lift_hbm, bias_hbm, conv_hbm,
+    hid_ref, lat_ref, dec_ref,
+    q_ref, k_ref, v_ref, stream_ref, gain_ref, lw_ref, place_ref,
     qkv, obuf, att, part, part_in,
     tiles, lifts, biases, taps, act1, act2, feat, acc,
+    ready, ready_mate,
     send_sem, recv_sem, osend_sem, orecv_sem, psend_sem, precv_sem,
-    load_sem, hid_sem, tap_sem, dsend_sem, drecv_sem,
+    load_sem, side_sem, tap_sem, dsend_sem, drecv_sem,
 ):
-    loads = [
-        pltpu.make_async_copy(source, target, load_sem.at[i])
-        for i, (source, target) in enumerate(
-            ((q_hbm, q_ref), (k_hbm, k_ref), (v_hbm, v_ref), (stream_hbm, stream_ref))
-        )
-    ]
-    for load in loads:
-        load.start()
     seq, rep, head = (lax.axis_index(a) for a in ("seq", "rep", "head"))
     count = seq_size * rep_size
     me = seq * rep_size + rep
@@ -136,27 +129,73 @@
     own_heads = qkv.shape[0]
     others = count - 1
     factor = 1.0 / math.sqrt(HEAD_DIM)
-    offsets = [(d, e) for d in (2, 1, 3, 0) for e in range(rep_size) if (d, e) != (0, 0)]
-
-    def peer(d, e):
-        return lax.rem(seq + d, seq_size), lax.rem(rep + e, rep_size)
-
-    partner = {"head": lax.rem(head + 1, head_size)}
-    mates = [
-        {"head": lax.rem(head + d, head_size), "rep": lax.rem(rep + e, rep_size)}
-        for d in range(head_size) for e in range(rep_size) if (d, e) != (0, 0)
+    quarter = head * rep_size + rep
+    sources = (q_ref, k_ref, v_ref)
+
+    stretch = count * HEAD_DIM
+    loads = []
+    for h in range(own_heads):
+        cols = pl.ds(h * stretch, stretch)
+        loads.append([
+            pltpu.make_async_copy(origin.at[:, cols], source.at[:, cols], load_sem.at[3 * h + i])
+            for i, (origin, source) in enumerate(zip((q_hbm, k_hbm, v_hbm), sources))
+        ])
+    for load in loads[0]:
+        load.start()
+
+    barrier = pltpu.get_barrier_semaphore()
+    for e in range(1, rep_size):
+        pl.semaphore_signal(
+            barrier, inc=1, device_id={"rep": lax.rem(rep + e, rep_size)}, device_id_type=MESH
+        )
+    for k in range(1, seq_size):
+        @pl.when(seq + k < seq_size)
+        def _():
+            for r in range(rep_size):
+                pl.semaphore_signal(
+                    barrier, inc=1, device_id={"seq": seq + k, "rep": r}, device_id_type=MESH
+                )
+    for k in range(1, head_size):
+        @pl.when(head + k < head_size)
+        def _():
+            for r in range(rep_size):
+                pl.semaphore_signal(
+                    barrier, inc=1, device_id={"head": head + k, "rep": r}, device_id_type=MESH
+                )
+    pl.semaphore_wait(barrier, rep_size - 1 + rep_size * (seq + head))
+    for k in range(1, seq_size):
+        @pl.when(seq >= k)
+        def _():
+            for r in range(rep_size):
+                pl.semaphore_signal(
+                    ready.at[k - 1], inc=1, device_id={"seq": seq - k, "rep": r},
+                    device_id_type=MESH,
+                )
+    for k in range(1, head_size):
+        @pl.when(head >= k)
+        def _():
+            for r in range(rep_size):
+                pl.semaphore_signal(
+                    ready_mate.at[k - 1], inc=1, device_id={"head": head - k, "rep": r},
+                    device_id_type=MESH,
+                )
+
+    share = tiles.shape[1] // (head_size * rep_size)
+    my_share = pl.ds(pl.multiple_of(quarter * share, share), share)
+    sides = [
+        pltpu.make_async_copy(origin, target, side_sem.at[i])
+        for i, (origin, target) in enumerate((
+            (tile_hbm.at[0, my_share], tiles.at[seq, my_share]),
+            (lift_hbm, lifts.at[quarter]),
+            (bias_hbm, biases.at[quarter]),
+            (place_hbm, place_ref),
+            (stream_hbm, stream_ref),
+            (gain_hbm, gain_ref),
+            (lw_hbm, lw_ref),
+        ))
     ]
-    quarter = head * rep_size + rep
-    tap_copy = pltpu.make_async_copy(conv_ref, taps, tap_sem)
-    tap_copy.start()
-    barrier = pltpu.get_barrier_semaphore()
-    for d, e in offsets:
-        ps, pr = peer(d, e)
-        pl.semaphore_signal(barrier, inc=1, device_id={"seq": ps, "rep": pr}, device_id_type=MESH)
-    strangers = [m for m, e in zip(mates, range(1, head_size * rep_size)) if e >= rep_size]
-    for mate in strangers:
-        pl.semaphore_signal(barrier, inc=1, device_id=mate, device_id_type=MESH)
-    pl.semaphore_wait(barrier, others + len(strangers))
+    for side in sides[:4]:
+        side.start()
 
     def arrived(ref, sem):
         pltpu.make_async_copy(ref, ref, sem).wait()
@@ -168,51 +207,86 @@
             device_id=device, device_id_type=MESH,
         ).start()
 
-    share = tile_ref.shape[1] // (head_size * rep_size)
-    my_share = pl.ds(pl.multiple_of(quarter * share, share), share)
-    for d in range(1, seq_size):
-        send(tile_ref.at[0, my_share], tiles.at[seq, my_share], 0,
-             {"seq": lax.rem(seq + d, seq_size)})
+    my_rows = pl.ds(pl.multiple_of(me * rows, rows), rows)
+
+    def block_of(h, place):
+        return pl.ds(pl.multiple_of((h * count + place) * HEAD_DIM, HEAD_DIM), HEAD_DIM)
+
+    def send_one(h, target, r):
+        columns = block_of(h, target * rep_size + r)
+        for i, source in enumerate(sources):
+            pltpu.make_async_remote_copy(
+                src_ref=source.at[:, columns],
+                dst_ref=qkv.at[h, i, my_rows, :],
+                send_sem=send_sem,
+                recv_sem=recv_sem.at[h],
+                device_id={"seq": target, "rep": r},
+                device_id_type=MESH,
+            ).start()
+
+    def send_head(h):
+        for k in (2, 1, 3):
+            @pl.when(seq >= k)
+            def _():
+                if h == 0:
+                    send(tiles.at[seq, my_share], tiles.at[seq, my_share], 0, {"seq": seq - k})
+                for r in range(rep_size):
+                    send_one(h, seq - k, r)
+        for k in range(1, seq_size):
+            @pl.when(seq + k < seq_size)
+            def _():
+                if h == 0:
+                    pl.semaphore_wait(ready.at[k - 1], rep_size)
+                    send(tiles.at[seq, my_share], tiles.at[seq, my_share], 0, {"seq": seq + k})
+                for r in range(rep_size):
+                    send_one(h, seq + k, r)
+        for e in range(1, rep_size):
+            send_one(h, seq, lax.rem(rep + e, rep_size))
+
+    for load in loads[0]:
+        load.wait()
+    sides[0].wait()
+    send_head(0)
+    for pending in loads[1:]:
+        for load in pending:
+            load.start()
+    tap_copy = pltpu.make_async_copy(conv_hbm, taps, tap_sem)
+    tap_copy.start()
+    for side in sides[4:]:
+        side.start()
+    for h in range(1, own_heads):
+        for load in loads[h]:
+            load.wait()
+        send_head(h)
+
+    mates = [
+        {"head": lax.rem(head + d, head_size), "rep": lax.rem(rep + e, rep_size)}
+        for d in range(head_size) for e in range(rep_size) if (d, e) != (0, 0)
+    ]
+    for k in range(1, head_size):
+        @pl.when(head + k < head_size)
+        def _():
+            pl.semaphore_wait(ready_mate.at[k - 1], rep_size)
+    sides[1].wait()
+    sides[2].wait()
     for mate in mates:
-        send(lift_ref, lifts.at[quarter], 1, mate)
-        send(bias_ref, biases.at[quarter], 2, mate)
-
-    for load in loads[:3]:
-        load.wait()
-    my_rows = pl.ds(pl.multiple_of(me * rows, rows), rows)
-    sources = (q_ref, k_ref, v_ref)
-    for h in range(own_heads):
-        for d, e in offsets:
-            ps, pr = peer(d, e)
-            column = ((ps * rep_size + pr) * own_heads + h) * HEAD_DIM
-            columns = pl.ds(pl.multiple_of(column, HEAD_DIM), HEAD_DIM)
-            for a, source in enumerate(sources):
-                pltpu.make_async_remote_copy(
-                    src_ref=source.at[:, columns],
-                    dst_ref=qkv.at[h, a, my_rows, :],
-                    send_sem=send_sem,
-                    recv_sem=recv_sem.at[h],
-                    device_id={"seq": ps, "rep": pr},
-                    device_id_type=MESH,
-                ).start()
-    for h in range(own_heads):
-        columns = pl.ds(pl.multiple_of((me * own_heads + h) * HEAD_DIM, HEAD_DIM), HEAD_DIM)
-        for a, source in enumerate(sources):
-            qkv[h, a, my_rows, :] = source[:, columns]
-
-    tiles[seq, my_share] = tile_ref[0, my_share]
-    lifts[quarter] = lift_ref[...]
-    biases[quarter] = bias_ref[...]
+        send(lifts.at[quarter], lifts.at[quarter], 1, mate)
+        send(biases.at[quarter], biases.at[quarter], 2, mate)
     pieces = len(mates)
     arrived(tiles.at[pl.ds(0, seq_size - 1), pl.ds(0, share)], drecv_sem.at[0])
     for mate in mates:
         send(tiles.at[:, my_share], tiles.at[:, my_share], 3, mate)
+    for h in range(own_heads):
+        columns = block_of(h, me)
+        for i, source in enumerate(sources):
+            qkv[h, i, my_rows, :] = source[:, columns]
+    sides[3].wait()
     arrived(lifts.at[pl.ds(0, pieces)], drecv_sem.at[1])
     arrived(biases.at[pl.ds(0, pieces)], drecv_sem.at[2])
     arrived(tiles.at[:, pl.ds(0, pieces * share)], drecv_sem.at[3])
 
     frames, reach, columns_here, channels = act1.shape
-    own = lift_ref.shape[1]
+    own = lifts.shape[2]
     margin = reach // 2
     own_lanes = pl.ds(pl.multiple_of(quarter * own, own), own)
 
@@ -239,7 +313,7 @@
                 active = silu(lifted(chosen, lifts[c], biases[c])) * inside(d - margin)
                 act1[f, d, :, c * own:(c + 1) * own] = active.astype(jnp.bfloat16)
             if 1 <= d <= reach - 2:
-                feat[f, d - 1] = lifted(chosen, lift_ref[...], bias_ref[...])
+                feat[f, d - 1] = lifted(chosen, lifts[quarter], biases[quarter])
 
     def convolve(layer, active, rows_out):
         length = rows_out * columns_here
@@ -283,17 +357,23 @@
         arrived(act2.at[:, :, :, pl.ds(0, pieces * own)], drecv_sem.at[4])
         convolve(1, act2, reach - 4)
         for f in range(frames):
-            dec_ref[f * columns_here:(f + 1) * columns_here, :] = (
+            dec_ref[pl.ds(f, own, stride=frames), :] = jnp.transpose(
                 feat[f, margin - 1] + gathered_columns(f, 0)
             )
+
+    half = seq_size // 2
+    upper = seq // half
+
+    def nearest(step):
+        return upper * (seq_size - 1 - step) + (1 - upper) * step
 
     block = rep_size * rows
     for h in range(own_heads):
         arrived(qkv.at[h, :, pl.ds(0, others * rows), :], recv_sem.at[h])
-        out_columns = pl.ds(pl.multiple_of((me * own_heads + h) * HEAD_DIM, HEAD_DIM), HEAD_DIM)
+        out_columns = block_of(h, me)
 
         def attend(step, carry):
-            target = lax.rem(seq + 2 + step, seq_size)
+            target = nearest(seq_size - 1 - step)
             here = pl.ds(pl.multiple_of(target * block, block), block)
             scores = lax.dot_general(
                 qkv[h, 0, here, :], qkv[h, 1], (((1,), (1,)), ((), ())),
@@ -313,7 +393,7 @@
                         src_ref=obuf.at[h, pl.ds(start, rows), :],
                         dst_ref=att.at[:, out_columns],
                         send_sem=osend_sem,
-                        recv_sem=orecv_sem.at[h],
+                        recv_sem=orecv_sem.at[h * count + me],
                         device_id={"seq": target, "rep": r},
                         device_id_type=MESH,
                     ).start()
@@ -321,77 +401,65 @@
 
         lax.fori_loop(0, seq_size, attend, 0)
         att[:, out_columns] = obuf[h, my_rows, :]
-        if h == own_heads - 1:
+        if h == 0:
             last_layer()
 
-    loads[3].wait()
+    for side in sides[4:]:
+        side.wait()
+    latent = lat_ref.shape[0]
     squares = jnp.zeros((rows, HEAD_DIM), jnp.float32)
-    projected = jnp.zeros((rows, lw_ref.shape[0]), jnp.float32)
+    projected = jnp.zeros((latent, rows), jnp.float32)
     for h in range(own_heads):
-        arrived(obuf.at[h, pl.ds(0, others * rows), :], orecv_sem.at[h])
-        for j in range(count):
-            low = (j * own_heads + h) * HEAD_DIM
-            cols = slice(low, low + HEAD_DIM)
-            combined = stream_ref[:, cols].astype(jnp.float32) + att[:, cols].astype(jnp.float32)
-            hidden = combined.astype(jnp.bfloat16)
-            hid_ref[:, cols] = hidden
-            widened = hidden.astype(jnp.float32)
-            squares = squares + widened * widened
-            scaled = (widened * gain_ref[:, cols]).astype(jnp.bfloat16)
-            projected = projected + lax.dot_general(
-                scaled, lw_ref[:, cols], (((1,), (1,)), ((), ())),
-                preferred_element_type=jnp.float32,
-            )
-    latent = projected.shape[1]
-    summed = jnp.sum(squares, axis=1, keepdims=True)
-    part[:, :latent] = projected
-    part[:, latent:] = jnp.broadcast_to(summed, (rows, part.shape[1] - latent))
+        for step in range(seq_size):
+            for r in range(rep_size):
+                origin = nearest(step) * rep_size + r
+
+                @pl.when(origin != me)
+                def _():
+                    arrived(obuf.at[h, pl.ds(0, rows), :], orecv_sem.at[h * count + origin])
+
+                cols = block_of(h, origin)
+                combined = (
+                    stream_ref[:, cols].astype(jnp.float32) + att[:, cols].astype(jnp.float32)
+                )
+                hidden = combined.astype(jnp.bfloat16)
+                hid_ref[:, cols] = hidden
+                widened = hidden.astype(jnp.float32)
+                squares = squares + widened * widened
+                scaled = (widened * gain_ref[:, cols]).astype(jnp.bfloat16)
+                projected = projected + lax.dot_general(
+                    lw_ref[:, cols], scaled, (((1,), (1,)), ((), ())),
+                    preferred_element_type=jnp.float32,
+                )
+    summed = jnp.sum(jnp.transpose(squares), axis=0, keepdims=True)
+    part[:latent] = projected.astype(jnp.bfloat16)
+    part[latent:] = jnp.broadcast_to(summed, (part.shape[0] - latent, rows)).astype(jnp.bfloat16)
     swap = pltpu.make_async_remote_copy(
         src_ref=part, dst_ref=part_in, send_sem=psend_sem, recv_sem=precv_sem,
-        device_id=partner, device_id_type=MESH,
+        device_id={"head": lax.rem(head + 1, head_size)}, device_id_type=MESH,
     )
     swap.start()
-    hid_copy = pltpu.make_async_copy(hid_ref, hid_hbm, hid_sem)
-    hid_copy.start()
     arrived(qkv.at[:, :, pl.ds(0, others * rows), :], send_sem)
     arrived(obuf.at[:, pl.ds(0, others * rows), :], osend_sem)
-    swap.wait()
     arrived(tiles.at[pl.ds(0, seq_size - 1), pl.ds(0, share)], dsend_sem.at[0])
     arrived(lifts.at[pl.ds(0, pieces)], dsend_sem.at[1])
     arrived(biases.at[pl.ds(0, pieces)], dsend_sem.at[2])
     arrived(tiles.at[:, pl.ds(0, pieces * share)], dsend_sem.at[3])
     arrived(act2.at[:, :, :, pl.ds(0, pieces * own)], dsend_sem.at[4])
-    sums_ref[...] = part[...] + part_in[...]
-    hid_copy.wait()
-
-
-def finish_kernel(
-    full_width, hid_in, sums_ref, dec_in, hid_out, lat_ref, dec_ref, held, in_sem, out_sem
-):
-    chunks = held.shape[0]
-    size = hid_in.shape[0] // chunks
-    reads = [
-        pltpu.make_async_copy(hid_in.at[pl.ds(i * size, size), :], held.at[i], in_sem.at[i])
-        for i in range(chunks)
+    swap.wait()
+    both = part[...].astype(jnp.float32) + part_in[...].astype(jnp.float32)
+    lat_ref[...] = both[:latent] * lax.rsqrt(both[latent:latent + 1] / full_width + epsilon)
+
+
+def finish_kernel(hid_in, lat_in, dec_in, hid_out, lat_out, dec_out, sem):
+    writes = [
+        pltpu.make_async_copy(held, out, sem.at[i])
+        for i, (held, out) in enumerate(
+            ((hid_in, hid_out), (lat_in, lat_out), (dec_in, dec_out))
+        )
     ]
-    writes = [
-        pltpu.make_async_copy(held.at[i], hid_out.at[pl.ds(i * size, size), :], out_sem.at[i])
-        for i in range(chunks)
-    ]
-    for read in reads:
-        read.start()
-    for read, write in zip(reads, writes):
-        read.wait()
+    for write in writes:
         write.start()
-    latent = lat_ref.shape[0]
-    sums = jnp.transpose(sums_ref[...])
-    lat_ref[...] = sums[:latent] * lax.rsqrt(sums[latent:latent + 1] / full_width + epsilon)
-    frames = dec_ref.shape[0] // dec_in.shape[1]
-    columns = dec_in.shape[0] // frames
-    for f in range(frames):
-        dec_ref[pl.ds(f, dec_in.shape[1], stride=frames), :] = jnp.transpose(
-            dec_in[f * columns:(f + 1) * columns, :]
-        )
     for write in writes:
         write.wait()
 
@@ -405,7 +473,6 @@
     count = seq_size * rep_size
     own_heads = width // HEAD_DIM // count
     latent = latent_weight.shape[1]
-    lanes = 2 * latent
     depth, frames, columns = tile_pool.shape[1:]
     layers, _, own, channels = conv_weight.shape
     quarters = head_size * rep_size
@@ -413,23 +480,26 @@
     bf = jnp.bfloat16
     vmem = pl.BlockSpec(memory_space=pltpu.VMEM)
     hbm = pl.BlockSpec(memory_space=pltpu.HBM)
-    smem = pl.BlockSpec(memory_space=pltpu.SMEM)
     dma = pltpu.SemaphoreType.DMA
-    hidden, sums, decoded = pl.pallas_call(
-        functools.partial(fused_kernel, seq_size, rep_size, head_size),
-        out_shape=(
-            jax.ShapeDtypeStruct((rows, width), bf),
-            jax.ShapeDtypeStruct((rows, lanes), jnp.float32),
-            jax.ShapeDtypeStruct((frames * columns, own), jnp.float32),
-        ),
-        in_specs=[hbm] * 4 + [vmem] * 3 + [smem, vmem, vmem, hbm],
-        out_specs=(hbm, vmem, vmem),
-        scratch_shapes=[pltpu.VMEM((rows, width), bf)] * 5 + [
+    held = (
+        pltpu.VMEM((rows, width), bf),
+        pltpu.VMEM((latent, rows), jnp.float32),
+        pltpu.VMEM((own * frames, columns), jnp.float32),
+    )
+    hidden, latents, decoded = pl.pallas_call(
+        functools.partial(fused_kernel, seq_size, rep_size, head_size, width * head_size),
+        out_shape=held,
+        in_specs=[hbm] * 11,
+        out_specs=(vmem, vmem, vmem),
+        scratch_shapes=[pltpu.VMEM((rows, width), bf)] * 4 + [
+            pltpu.VMEM((1, width), jnp.float32),
+            pltpu.VMEM((latent, width), bf),
+            pltpu.SMEM(tile_position.shape, jnp.int32),
             pltpu.VMEM((own_heads, 3, count * rows, HEAD_DIM), bf),
             pltpu.VMEM((own_heads, count * rows, HEAD_DIM), bf),
             pltpu.VMEM((rows, width), bf),
-            pltpu.VMEM((rows, lanes), jnp.float32),
-            pltpu.VMEM((rows, lanes), jnp.float32),
+            pltpu.VMEM((latent + 16, rows), bf),
+            pltpu.VMEM((latent + 16, rows), bf),
             pltpu.VMEM((seq_size, depth, frames, columns), bf),
             pltpu.VMEM((quarters, depth, own), bf),
             pltpu.VMEM((quarters, 1, own), jnp.float32),
@@ -438,30 +508,28 @@
             pltpu.VMEM((frames, reach - 2, columns, channels), bf),
             pltpu.VMEM((frames, reach - 2, columns, own), jnp.float32),
             pltpu.VMEM((frames, (reach - 2) * columns, 3 * own), jnp.float32),
-            dma, dma((own_heads,)), dma, dma((own_heads,)), dma, dma,
-            dma((4,)), dma, dma, dma((5,)), dma((5,)),
+            pltpu.SemaphoreType.REGULAR((seq_size - 1,)),
+            pltpu.SemaphoreType.REGULAR((head_size - 1,)),
+            dma, dma((own_heads,)), dma, dma((own_heads * count,)), dma, dma,
+            dma((3 * own_heads,)), dma((7,)), dma, dma((5,)), dma((5,)),
         ],
         compiler_params=pltpu.CompilerParams(
-            collective_id=0, has_side_effects=True, vmem_limit_bytes=56 << 20
+            collective_id=0, has_side_effects=True, vmem_limit_bytes=48 << 20
         ),
-    )(
-        queries, key_tokens, value_tokens, stream, norm_gain[None, :], latent_weight.T,
-        tile_pool, tile_position, lift_weight, lift_bias[None, :], conv_weight,
-    )
-    chunks = 4
+    )(*(
+        pltpu.with_memory_space_constraint(operand, pltpu.HBM) for operand in (
+            queries, key_tokens, value_tokens, stream, norm_gain[None, :], latent_weight.T,
+            tile_pool, tile_position, lift_weight, lift_bias[None, :], conv_weight,
+        )
+    ))
     hidden, latents, decoded = pl.pallas_call(
-        functools.partial(finish_kernel, width * head_size),
-        out_shape=(
-            jax.ShapeDtypeStruct((rows, width), bf),
-            jax.ShapeDtypeStruct((latent, rows), jnp.float32),
-            jax.ShapeDtypeStruct((own * frames, columns), jnp.float32),
-        ),
-        in_specs=[hbm, vmem, vmem],
-        out_specs=(hbm, vmem, vmem),
-        scratch_shapes=[
-            pltpu.VMEM((chunks, rows // chunks, width), bf), dma((chunks,)), dma((chunks,)),
-        ],
-    )(hidden, sums, decoded)
+        finish_kernel,
+        out_shape=tuple(jax.ShapeDtypeStruct(ref.shape, ref.dtype) for ref in held),
+        in_specs=[vmem, vmem, vmem],
+        out_specs=(hbm, hbm, hbm),
+        scratch_shapes=[dma((3,))],
+        compiler_params=pltpu.CompilerParams(vmem_limit_bytes=8 << 20),
+    )(hidden, latents, decoded)
     return hidden, latents.T, decoded.reshape(own, frames, 1, columns)
 
 

time: 84.1 us -> 79 us (0.939)
  Pallas kernels: 83.2 us -> 78.2 us
    pallas_call x1, Pallas kernels: 3.57 us -> 0.95 us  [fused(): pl.pallas_call(finish_kernel, out_shape=tuple((jax.ShapeDtypeStruct(ref.s...]
    pallas_call x1, Pallas kernels: 79.7 us -> 77.3 us  [fused(): pl.pallas_call(functools.partial(fused_kernel, seq_size, rep_size, head_s...]
where the time goes in v1:
time: 79 us; the launch traced here: 78.9 us
  Pallas kernels  78.2 us (99%)
    pallas_call x1, Pallas kernels, fused(): pl.pallas_call(functools.partial(fused_kernel, seq_size, rep_size, head_s...  77.3 us

profile of v1, /device:TPU:0, one launch (start us, length us, event | category | flops | bytes accessed | tf_op | source)
XLA Modules:
  0.0 78.9 jit_solution(5150756490332944759)
XLA Ops:
  0.6 77.3 %shard_map.130 = (bf16[128,3072]{1,0:T(8,128)(2,1)S(1)}, f32[64,128]{1,0:T(8,128)S(1)}, f32[256,128]{1,0:T(8,128)S(1)}) custom-call(bf16[128,3072]{1,0:T(8,128)(2,1)} %q_hbm.1, bf16[128,3072]{1,0:T(8,128)(2,1)} %k_hbm.1, bf16[128,3072]{1,0:T(8,128)(2,1)} %v_hbm.1, bf16[128,3072]{1,0:T(8,128)(2,1)} %stream_hbm.1, f32[1,3072]{1,0:T(1,128)} %bitcast.8, ...), custom_call_target="tpu_custom_call" | custom-call | tf_op jit(solution)/shard_map/pallas_call | solution.py:489
  77.9 1.0 %shard_map.131 = (bf16[128,3072]{1,0:T(8,128)(2,1)}, f32[64,128]{1,0:T(8,128)}, f32[256,128]{1,0:T(8,128)}) custom-call(bf16[128,3072]{1,0:T(8,128)(2,1)S(1)} %get-tuple-element.9.hid_in, f32[64,128]{1,0:T(8,128)S(1)} %get-tuple-element.10.lat_in, f32[256,128]{1,0:T(8,128)S(1)} %get-tuple-element.11.dec_in), custom_call_target="tpu_custom_call" | custom-call | tf_op jit(solution)/shard_map/pallas_call | solution.py:525

commit v2 on v1

--- a/solution.py
+++ b/solution.py
@@ -180,8 +180,13 @@
                     device_id_type=MESH,
                 )
 
-    share = tiles.shape[1] // (head_size * rep_size)
-    my_share = pl.ds(pl.multiple_of(quarter * share, share), share)
+    half = seq_size // 2
+    upper = seq // half
+    far = (1 - upper) * half
+    inner = upper * half + (1 - upper) * (half - 1)
+    mirror = 2 * half * upper + half - 1 - seq
+    share = tiles.shape[1] // rep_size
+    my_share = pl.ds(pl.multiple_of(rep * share, share), share)
     sides = [
         pltpu.make_async_copy(origin, target, side_sem.at[i])
         for i, (origin, target) in enumerate((
@@ -194,8 +199,10 @@
             (lw_hbm, lw_ref),
         ))
     ]
-    for side in sides[:4]:
-        side.start()
+    @pl.when(head == 0)
+    def _():
+        sides[0].start()
+
 
     def arrived(ref, sem):
         pltpu.make_async_copy(ref, ref, sem).wait()
@@ -212,52 +219,71 @@
     def block_of(h, place):
         return pl.ds(pl.multiple_of((h * count + place) * HEAD_DIM, HEAD_DIM), HEAD_DIM)
 
-    def send_one(h, target, r):
-        columns = block_of(h, target * rep_size + r)
-        for i, source in enumerate(sources):
-            pltpu.make_async_remote_copy(
-                src_ref=source.at[:, columns],
-                dst_ref=qkv.at[h, i, my_rows, :],
-                send_sem=send_sem,
-                recv_sem=recv_sem.at[h],
-                device_id={"seq": target, "rep": r},
-                device_id_type=MESH,
-            ).start()
-
-    def send_head(h):
+    def send_one(h, i, target, r):
+        pltpu.make_async_remote_copy(
+            src_ref=sources[i].at[:, block_of(h, target * rep_size + r)],
+            dst_ref=qkv.at[h, i, my_rows, :],
+            send_sem=send_sem,
+            recv_sem=recv_sem.at[h],
+            device_id={"seq": target, "rep": r},
+            device_id_type=MESH,
+        ).start()
+
+    def send_back(h, arrays):
         for k in (2, 1, 3):
             @pl.when(seq >= k)
             def _():
-                if h == 0:
-                    send(tiles.at[seq, my_share], tiles.at[seq, my_share], 0, {"seq": seq - k})
                 for r in range(rep_size):
-                    send_one(h, seq - k, r)
+                    for i in arrays:
+                        send_one(h, i, seq - k, r)
+
+    def send_on(h):
         for k in range(1, seq_size):
             @pl.when(seq + k < seq_size)
             def _():
                 if h == 0:
                     pl.semaphore_wait(ready.at[k - 1], rep_size)
-                    send(tiles.at[seq, my_share], tiles.at[seq, my_share], 0, {"seq": seq + k})
                 for r in range(rep_size):
-                    send_one(h, seq + k, r)
+                    for i in range(3):
+                        send_one(h, i, seq + k, r)
         for e in range(1, rep_size):
-            send_one(h, seq, lax.rem(rep + e, rep_size))
-
-    for load in loads[0]:
+            for i in range(3):
+                send_one(h, i, seq, lax.rem(rep + e, rep_size))
+
+    own_tile = tiles.at[seq, my_share]
+    far_tiles = tiles.at[pl.ds(far, half), my_share]
+    for i, load in enumerate(loads[0]):
         load.wait()
-    sides[0].wait()
-    send_head(0)
+        send_back(0, (i,))
     for pending in loads[1:]:
         for load in pending:
             load.start()
+    send_on(0)
+
+    @pl.when(head == 0)
+    def _():
+        sides[0].wait()
+        send(own_tile, own_tile, 0, {"seq": mirror})
+        send(own_tile, own_tile, 0, {"seq": (1 - upper) * half + upper * (half - 1)})
+
+        @pl.when(seq == inner)
+        def _():
+            arrived(tiles.at[pl.ds(0, seq_size - 1), pl.ds(0, share)], drecv_sem.at[0])
+            pltpu.make_async_remote_copy(
+                src_ref=far_tiles, dst_ref=far_tiles,
+                send_sem=dsend_sem.at[5], recv_sem=drecv_sem.at[0],
+                device_id={"seq": mirror}, device_id_type=MESH,
+            ).start()
+
     tap_copy = pltpu.make_async_copy(conv_hbm, taps, tap_sem)
     tap_copy.start()
-    for side in sides[4:]:
+    for side in sides[1:]:
         side.start()
     for h in range(1, own_heads):
         for load in loads[h]:
             load.wait()
-        send_head(h)
+        send_back(h, range(3))
+        send_on(h)
 
     mates = [
         {"head": lax.rem(head + d, head_size), "rep": lax.rem(rep + e, rep_size)}
@@ -273,9 +299,15 @@
         send(lifts.at[quarter], lifts.at[quarter], 1, mate)
         send(biases.at[quarter], biases.at[quarter], 2, mate)
     pieces = len(mates)
-    arrived(tiles.at[pl.ds(0, seq_size - 1), pl.ds(0, share)], drecv_sem.at[0])
-    for mate in mates:
-        send(tiles.at[:, my_share], tiles.at[:, my_share], 3, mate)
+    @pl.when(head == 0)
+    def _():
+        @pl.when(seq != inner)
+        def _():
+            arrived(tiles.at[pl.ds(0, seq_size - 1), pl.ds(0, share)], drecv_sem.at[0])
+
+        for mate in mates:
+            send(tiles.at[:, my_share], tiles.at[:, my_share], 3, mate)
+
     for h in range(own_heads):
         columns = block_of(h, me)
         for i, source in enumerate(sources):
@@ -283,7 +315,13 @@
     sides[3].wait()
     arrived(lifts.at[pl.ds(0, pieces)], drecv_sem.at[1])
     arrived(biases.at[pl.ds(0, pieces)], drecv_sem.at[2])
-    arrived(tiles.at[:, pl.ds(0, pieces * share)], drecv_sem.at[3])
+    @pl.when(head == 0)
+    def _():
+        arrived(tiles.at[:, pl.ds(0, (rep_size - 1) * share)], drecv_sem.at[3])
+
+    @pl.when(head != 0)
+    def _():
+        arrived(tiles, drecv_sem.at[3])
 
     frames, reach, columns_here, channels = act1.shape
     own = lifts.shape[2]
@@ -361,19 +399,23 @@
                 feat[f, margin - 1] + gathered_columns(f, 0)
             )
 
-    half = seq_size // 2
-    upper = seq // half
-
-    def nearest(step):
-        return upper * (seq_size - 1 - step) + (1 - upper) * step
+    def give(h, target, r):
+        start = pl.multiple_of(target * block + r * rows, rows)
+        pltpu.make_async_remote_copy(
+            src_ref=obuf.at[h, pl.ds(start, rows), :],
+            dst_ref=att.at[:, block_of(h, me)],
+            send_sem=osend_sem,
+            recv_sem=orecv_sem.at[h * count + me],
+            device_id={"seq": target, "rep": r},
+            device_id_type=MESH,
+        ).start()
 
     block = rep_size * rows
     for h in range(own_heads):
         arrived(qkv.at[h, :, pl.ds(0, others * rows), :], recv_sem.at[h])
-        out_columns = block_of(h, me)
 
         def attend(step, carry):
-            target = nearest(seq_size - 1 - step)
+            target = lax.rem(far + step, seq_size)
             here = pl.ds(pl.multiple_of(target * block, block), block)
             scores = lax.dot_general(
                 qkv[h, 0, here, :], qkv[h, 1], (((1,), (1,)), ((), ())),
@@ -386,21 +428,23 @@
             )
             obuf[h, here, :] = (summed / total).astype(jnp.bfloat16)
             for r in range(rep_size):
-                @pl.when(jnp.logical_or(target != seq, rep != r))
+                other = jnp.logical_or(target != seq, rep != r)
+                if r == rep_size - 1:
+                    if h < own_heads - 1:
+                        other = jnp.logical_and(other, step != 1)
+                    else:
+                        @pl.when(step == 1)
+                        def _():
+                            for e in range(own_heads - 1):
+                                give(e, target, r)
+
+                @pl.when(other)
                 def _():
-                    start = pl.multiple_of(target * block + r * rows, rows)
-                    pltpu.make_async_remote_copy(
-                        src_ref=obuf.at[h, pl.ds(start, rows), :],
-                        dst_ref=att.at[:, out_columns],
-                        send_sem=osend_sem,
-                        recv_sem=orecv_sem.at[h * count + me],
-                        device_id={"seq": target, "rep": r},
-                        device_id_type=MESH,
-                    ).start()
+                    give(h, target, r)
             return carry
 
         lax.fori_loop(0, seq_size, attend, 0)
-        att[:, out_columns] = obuf[h, my_rows, :]
+        att[:, block_of(h, me)] = obuf[h, my_rows, :]
         if h == 0:
             last_layer()
 
@@ -409,28 +453,30 @@
     latent = lat_ref.shape[0]
     squares = jnp.zeros((rows, HEAD_DIM), jnp.float32)
     projected = jnp.zeros((latent, rows), jnp.float32)
-    for h in range(own_heads):
-        for step in range(seq_size):
-            for r in range(rep_size):
-                origin = nearest(step) * rep_size + r
-
-                @pl.when(origin != me)
-                def _():
-                    arrived(obuf.at[h, pl.ds(0, rows), :], orecv_sem.at[h * count + origin])
-
-                cols = block_of(h, origin)
-                combined = (
-                    stream_ref[:, cols].astype(jnp.float32) + att[:, cols].astype(jnp.float32)
-                )
-                hidden = combined.astype(jnp.bfloat16)
-                hid_ref[:, cols] = hidden
-                widened = hidden.astype(jnp.float32)
-                squares = squares + widened * widened
-                scaled = (widened * gain_ref[:, cols]).astype(jnp.bfloat16)
-                projected = projected + lax.dot_general(
-                    lw_ref[:, cols], scaled, (((1,), (1,)), ((), ())),
-                    preferred_element_type=jnp.float32,
-                )
+    for h, step in [
+        (h, half * across + step)
+        for across in (1, 0) for h in range(own_heads) for step in range(half)
+    ]:
+        for r in range(rep_size):
+            origin = lax.rem(far + step, seq_size) * rep_size + r
+
+            @pl.when(origin != me)
+            def _():
+                arrived(obuf.at[h, pl.ds(0, rows), :], orecv_sem.at[h * count + origin])
+
+            cols = block_of(h, origin)
+            combined = (
+                stream_ref[:, cols].astype(jnp.float32) + att[:, cols].astype(jnp.float32)
+            )
+            hidden = combined.astype(jnp.bfloat16)
+            hid_ref[:, cols] = hidden
+            widened = hidden.astype(jnp.float32)
+            squares = squares + widened * widened
+            scaled = (widened * gain_ref[:, cols]).astype(jnp.bfloat16)
+            projected = projected + lax.dot_general(
+                lw_ref[:, cols], scaled, (((1,), (1,)), ((), ())),
+                preferred_element_type=jnp.float32,
+            )
     summed = jnp.sum(jnp.transpose(squares), axis=0, keepdims=True)
     part[:latent] = projected.astype(jnp.bfloat16)
     part[latent:] = jnp.broadcast_to(summed, (part.shape[0] - latent, rows)).astype(jnp.bfloat16)
@@ -441,10 +487,19 @@
     swap.start()
     arrived(qkv.at[:, :, pl.ds(0, others * rows), :], send_sem)
     arrived(obuf.at[:, pl.ds(0, others * rows), :], osend_sem)
-    arrived(tiles.at[pl.ds(0, seq_size - 1), pl.ds(0, share)], dsend_sem.at[0])
     arrived(lifts.at[pl.ds(0, pieces)], dsend_sem.at[1])
     arrived(biases.at[pl.ds(0, pieces)], dsend_sem.at[2])
-    arrived(tiles.at[:, pl.ds(0, pieces * share)], dsend_sem.at[3])
+
+    @pl.when(head == 0)
+    def _():
+        arrived(tiles.at[pl.ds(0, 2), pl.ds(0, share)], dsend_sem.at[0])
+        told = pieces * seq_size * share * frames * columns_here // HEAD_DIM
+        arrived(obuf.at[0, pl.ds(0, told), :], dsend_sem.at[3])
+
+        @pl.when(seq == inner)
+        def _():
+            arrived(far_tiles, dsend_sem.at[5])
+
     arrived(act2.at[:, :, :, pl.ds(0, pieces * own)], dsend_sem.at[4])
     swap.wait()
     both = part[...].astype(jnp.float32) + part_in[...].astype(jnp.float32)
@@ -511,7 +566,7 @@
             pltpu.SemaphoreType.REGULAR((seq_size - 1,)),
             pltpu.SemaphoreType.REGULAR((head_size - 1,)),
             dma, dma((own_heads,)), dma, dma((own_heads * count,)), dma, dma,
-            dma((3 * own_heads,)), dma((7,)), dma, dma((5,)), dma((5,)),
+            dma((3 * own_heads,)), dma((7,)), dma, dma((6,)), dma((5,)),
         ],
         compiler_params=pltpu.CompilerParams(
             collective_id=0, has_side_effects=True, vmem_limit_bytes=48 << 20

time: 79 us -> 76.7 us (0.971)
  Pallas kernels: 78.2 us -> 75.3 us
    pallas_call x1, Pallas kernels: 77.3 us -> 74.4 us  [fused(): pl.pallas_call(functools.partial(fused_kernel, seq_size, rep_size, head_s...]
where the time goes in v2:
time: 76.7 us; the launch traced here: 76 us
  Pallas kernels  75.3 us (98%)
    pallas_call x1, Pallas kernels, fused(): pl.pallas_call(functools.partial(fused_kernel, seq_size, rep_size, head_s...  74.4 us

profile of v2, /device:TPU:0, one launch (start us, length us, event | category | flops | bytes accessed | tf_op | source)
XLA Modules:
  0.0 76.0 jit_solution(14196297530278580968)
XLA Ops:
  0.6 74.4 %shard_map.130 = (bf16[128,3072]{1,0:T(8,128)(2,1)S(1)}, f32[64,128]{1,0:T(8,128)S(1)}, f32[256,128]{1,0:T(8,128)S(1)}) custom-call(bf16[128,3072]{1,0:T(8,128)(2,1)} %q_hbm.1, bf16[128,3072]{1,0:T(8,128)(2,1)} %k_hbm.1, bf16[128,3072]{1,0:T(8,128)(2,1)} %v_hbm.1, bf16[128,3072]{1,0:T(8,128)(2,1)} %stream_hbm.1, f32[1,3072]{1,0:T(1,128)} %bitcast.8, ...), custom_call_target="tpu_custom_call" | custom-call | tf_op jit(solution)/shard_map/pallas_call | solution.py:544
  75.0 1.0 %shard_map.131 = (bf16[128,3072]{1,0:T(8,128)(2,1)}, f32[64,128]{1,0:T(8,128)}, f32[256,128]{1,0:T(8,128)}) custom-call(bf16[128,3072]{1,0:T(8,128)(2,1)S(1)} %get-tuple-element.9.hid_in, f32[64,128]{1,0:T(8,128)S(1)} %get-tuple-element.10.lat_in, f32[256,128]{1,0:T(8,128)S(1)} %get-tuple-element.11.dec_in), custom_call_target="tpu_custom_call" | custom-call | tf_op jit(solution)/shard_map/pallas_call | solution.py:580

commit v3 on v2

--- a/solution.py
+++ b/solution.py
@@ -155,6 +155,15 @@
                 pl.semaphore_signal(
                     barrier, inc=1, device_id={"seq": seq + k, "rep": r}, device_id_type=MESH
                 )
+    half = seq_size // 2
+
+    @pl.when(seq == half)
+    def _():
+        for r in range(rep_size):
+            pl.semaphore_signal(
+                barrier, inc=1, device_id={"seq": seq - 1, "rep": r}, device_id_type=MESH
+            )
+
     for k in range(1, head_size):
         @pl.when(head + k < head_size)
         def _():
@@ -162,9 +171,10 @@
                 pl.semaphore_signal(
                     barrier, inc=1, device_id={"head": head + k, "rep": r}, device_id_type=MESH
                 )
-    pl.semaphore_wait(barrier, rep_size - 1 + rep_size * (seq + head))
+    greeted = seq + head + jnp.where(seq == half - 1, 1, 0)
+    pl.semaphore_wait(barrier, rep_size - 1 + rep_size * greeted)
     for k in range(1, seq_size):
-        @pl.when(seq >= k)
+        @pl.when(jnp.logical_and(seq >= k, jnp.logical_or(k > 1, seq != half)))
         def _():
             for r in range(rep_size):
                 pl.semaphore_signal(
@@ -180,7 +190,6 @@
                     device_id_type=MESH,
                 )
 
-    half = seq_size // 2
     upper = seq // half
     far = (1 - upper) * half
     inner = upper * half + (1 - upper) * (half - 1)
@@ -242,7 +251,10 @@
             @pl.when(seq + k < seq_size)
             def _():
                 if h == 0:
-                    pl.semaphore_wait(ready.at[k - 1], rep_size)
+                    @pl.when(jnp.logical_or(k > 1, seq != half - 1))
+                    def _():
+                        pl.semaphore_wait(ready.at[k - 1], rep_size)
+
                 for r in range(rep_size):
                     for i in range(3):
                         send_one(h, i, seq + k, r)
@@ -266,15 +278,6 @@
         send(own_tile, own_tile, 0, {"seq": mirror})
         send(own_tile, own_tile, 0, {"seq": (1 - upper) * half + upper * (half - 1)})
 
-        @pl.when(seq == inner)
-        def _():
-            arrived(tiles.at[pl.ds(0, seq_size - 1), pl.ds(0, share)], drecv_sem.at[0])
-            pltpu.make_async_remote_copy(
-                src_ref=far_tiles, dst_ref=far_tiles,
-                send_sem=dsend_sem.at[5], recv_sem=drecv_sem.at[0],
-                device_id={"seq": mirror}, device_id_type=MESH,
-            ).start()
-
     tap_copy = pltpu.make_async_copy(conv_hbm, taps, tap_sem)
     tap_copy.start()
     for side in sides[1:]:
@@ -285,6 +288,17 @@
         send_back(h, range(3))
         send_on(h)
 
+    @pl.when(head == 0)
+    def _():
+        @pl.when(seq == inner)
+        def _():
+            arrived(tiles.at[pl.ds(0, seq_size - 1), pl.ds(0, share)], drecv_sem.at[0])
+            pltpu.make_async_remote_copy(
+                src_ref=far_tiles, dst_ref=far_tiles,
+                send_sem=dsend_sem.at[5], recv_sem=drecv_sem.at[0],
+                device_id={"seq": mirror}, device_id_type=MESH,
+            ).start()
+
     mates = [
         {"head": lax.rem(head + d, head_size), "rep": lax.rem(rep + e, rep_size)}
         for d in range(head_size) for e in range(rep_size) if (d, e) != (0, 0)
@@ -299,30 +313,10 @@
         send(lifts.at[quarter], lifts.at[quarter], 1, mate)
         send(biases.at[quarter], biases.at[quarter], 2, mate)
     pieces = len(mates)
-    @pl.when(head == 0)
-    def _():
-        @pl.when(seq != inner)
-        def _():
-            arrived(tiles.at[pl.ds(0, seq_size - 1), pl.ds(0, share)], drecv_sem.at[0])
-
-        for mate in mates:
-            send(tiles.at[:, my_share], tiles.at[:, my_share], 3, mate)
-
     for h in range(own_heads):
         columns = block_of(h, me)
         for i, source in enumerate(sources):
             qkv[h, i, my_rows, :] = source[:, columns]
-    sides[3].wait()
-    arrived(lifts.at[pl.ds(0, pieces)], drecv_sem.at[1])
-    arrived(biases.at[pl.ds(0, pieces)], drecv_sem.at[2])
-    @pl.when(head == 0)
-    def _():
-        arrived(tiles.at[:, pl.ds(0, (rep_size - 1) * share)], drecv_sem.at[3])
-
-    @pl.when(head != 0)
-    def _():
-        arrived(tiles, drecv_sem.at[3])
-
     frames, reach, columns_here, channels = act1.shape
     own = lifts.shape[2]
     margin = reach // 2
@@ -339,19 +333,6 @@
         return lax.dot_general(
             chosen, weight, (((0,), (0,)), ((), ())), preferred_element_type=jnp.float32
         ) + bias
-
-    wide = [tiles[p].astype(jnp.float32) for p in range(seq_size)]
-    for d in range(reach):
-        picked = jnp.zeros(wide[0].shape, jnp.float32)
-        for p in range(seq_size):
-            picked = picked + jnp.where(place_ref[p] == seq + d - margin, 1.0, 0.0) * wide[p]
-        for f in range(frames):
-            chosen = picked[:, f, :].astype(jnp.bfloat16)
-            for c in range(pieces + 1):
-                active = silu(lifted(chosen, lifts[c], biases[c])) * inside(d - margin)
-                act1[f, d, :, c * own:(c + 1) * own] = active.astype(jnp.bfloat16)
-            if 1 <= d <= reach - 2:
-                feat[f, d - 1] = lifted(chosen, lifts[quarter], biases[quarter])
 
     def convolve(layer, active, rows_out):
         length = rows_out * columns_here
@@ -381,15 +362,49 @@
             + jnp.where(at == columns_here - 1, 0.0, after)
         )
 
-    tap_copy.wait()
-    convolve(0, act1, reach - 2)
-    for f in range(frames):
-        for r in range(reach - 2):
-            value = feat[f, r] + gathered_columns(f, r)
-            feat[f, r] = value
-            act2[f, r, :, own_lanes] = (silu(value) * inside(r + 1 - margin)).astype(jnp.bfloat16)
-    for mate in mates:
-        send(act2.at[:, :, :, own_lanes], act2.at[:, :, :, own_lanes], 4, mate)
+    def first_layer():
+        @pl.when(head == 0)
+        def _():
+            @pl.when(seq != inner)
+            def _():
+                arrived(tiles.at[pl.ds(0, seq_size - 1), pl.ds(0, share)], drecv_sem.at[0])
+
+            for mate in mates:
+                send(tiles.at[:, my_share], tiles.at[:, my_share], 3, mate)
+
+        sides[3].wait()
+        arrived(lifts.at[pl.ds(0, pieces)], drecv_sem.at[1])
+        arrived(biases.at[pl.ds(0, pieces)], drecv_sem.at[2])
+        @pl.when(head == 0)
+        def _():
+            arrived(tiles.at[:, pl.ds(0, (rep_size - 1) * share)], drecv_sem.at[3])
+
+        @pl.when(head != 0)
+        def _():
+            arrived(tiles, drecv_sem.at[3])
+
+        wide = [tiles[p].astype(jnp.float32) for p in range(seq_size)]
+        for d in range(reach):
+            picked = jnp.zeros(wide[0].shape, jnp.float32)
+            for p in range(seq_size):
+                picked = picked + jnp.where(place_ref[p] == seq + d - margin, 1.0, 0.0) * wide[p]
+            for f in range(frames):
+                chosen = picked[:, f, :].astype(jnp.bfloat16)
+                for c in range(pieces + 1):
+                    active = silu(lifted(chosen, lifts[c], biases[c])) * inside(d - margin)
+                    act1[f, d, :, c * own:(c + 1) * own] = active.astype(jnp.bfloat16)
+                if 1 <= d <= reach - 2:
+                    feat[f, d - 1] = lifted(chosen, lifts[quarter], biases[quarter])
+
+        tap_copy.wait()
+        convolve(0, act1, reach - 2)
+        for f in range(frames):
+            for r in range(reach - 2):
+                value = feat[f, r] + gathered_columns(f, r)
+                feat[f, r] = value
+                act2[f, r, :, own_lanes] = (silu(value) * inside(r + 1 - margin)).astype(jnp.bfloat16)
+        for mate in mates:
+            send(act2.at[:, :, :, own_lanes], act2.at[:, :, :, own_lanes], 4, mate)
 
     def last_layer():
         arrived(act2.at[:, :, :, pl.ds(0, pieces * own)], drecv_sem.at[4])
@@ -415,7 +430,9 @@
         arrived(qkv.at[h, :, pl.ds(0, others * rows), :], recv_sem.at[h])
 
         def attend(step, carry):
-            target = lax.rem(far + step, seq_size)
+            target = jnp.where(
+                step % 2 == 0, far + step // 2, jnp.where(step == 1, mirror, seq)
+            )
             here = pl.ds(pl.multiple_of(target * block, block), block)
             scores = lax.dot_general(
                 qkv[h, 0, here, :], qkv[h, 1], (((1,), (1,)), ((), ())),
@@ -427,16 +444,16 @@
                 exponent.astype(jnp.bfloat16), qkv[h, 2], preferred_element_type=jnp.float32
             )
             obuf[h, here, :] = (summed / total).astype(jnp.bfloat16)
+            inner_far = jnp.logical_and(step % 2 == 0, seq == inner)
             for r in range(rep_size):
                 other = jnp.logical_or(target != seq, rep != r)
-                if r == rep_size - 1:
-                    if h < own_heads - 1:
-                        other = jnp.logical_and(other, step != 1)
-                    else:
-                        @pl.when(step == 1)
-                        def _():
-                            for e in range(own_heads - 1):
-                                give(e, target, r)
+                if h < own_heads - 1:
+                    other = jnp.logical_and(other, jnp.logical_not(inner_far))
+                else:
+                    @pl.when(inner_far)
+                    def _():
+                        for e in range(own_heads - 1):
+                            give(e, target, r)
 
                 @pl.when(other)
                 def _():
@@ -446,6 +463,8 @@
         lax.fori_loop(0, seq_size, attend, 0)
         att[:, block_of(h, me)] = obuf[h, my_rows, :]
         if h == 0:
+            first_layer()
+        if h == 1:
             last_layer()
 
     for side in sides[4:]:

time: 76.7 us -> 75.6 us (0.986)
  Pallas kernels: 75.3 us -> 74.3 us
    pallas_call x1, Pallas kernels: 74.4 us -> 73.3 us  [fused(): pl.pallas_call(functools.partial(fused_kernel, seq_size, rep_size, head_s...]
where the time goes in v3:
time: 75.6 us; the launch traced here: 74.9 us
  Pallas kernels  74.3 us (98%)
    pallas_call x1, Pallas kernels, fused(): pl.pallas_call(functools.partial(fused_kernel, seq_size, rep_size, head_s...  73.3 us

profile of v3, /device:TPU:0, one launch (start us, length us, event | category | flops | bytes accessed | tf_op | source)
XLA Modules:
  0.0 74.9 jit_solution(16857991775571694741)
XLA Ops:
  0.6 73.3 %shard_map.130 = (bf16[128,3072]{1,0:T(8,128)(2,1)S(1)}, f32[64,128]{1,0:T(8,128)S(1)}, f32[256,128]{1,0:T(8,128)S(1)}) custom-call(bf16[128,3072]{1,0:T(8,128)(2,1)} %q_hbm.1, bf16[128,3072]{1,0:T(8,128)(2,1)} %k_hbm.1, bf16[128,3072]{1,0:T(8,128)(2,1)} %v_hbm.1, bf16[128,3072]{1,0:T(8,128)(2,1)} %stream_hbm.1, f32[1,3072]{1,0:T(1,128)} %bitcast.8, ...), custom_call_target="tpu_custom_call" | custom-call | tf_op jit(solution)/shard_map/pallas_call | solution.py:563
  74.0 1.0 %shard_map.131 = (bf16[128,3072]{1,0:T(8,128)(2,1)}, f32[64,128]{1,0:T(8,128)}, f32[256,128]{1,0:T(8,128)}) custom-call(bf16[128,3072]{1,0:T(8,128)(2,1)S(1)} %get-tuple-element.9.hid_in, f32[64,128]{1,0:T(8,128)S(1)} %get-tuple-element.10.lat_in, f32[256,128]{1,0:T(8,128)S(1)} %get-tuple-element.11.dec_in), custom_call_target="tpu_custom_call" | custom-call | tf_op jit(solution)/shard_map/pallas_call | solution.py:599

commit v4 on v3

--- a/solution.py
+++ b/solution.py
@@ -137,7 +137,7 @@
     for h in range(own_heads):
         cols = pl.ds(h * stretch, stretch)
         loads.append([
-            pltpu.make_async_copy(origin.at[:, cols], source.at[:, cols], load_sem.at[3 * h + i])
+            pltpu.make_async_copy(origin.at[:, cols], source.at[:, cols], load_sem.at[i if h == 0 else 3])
             for i, (origin, source) in enumerate(zip((q_hbm, k_hbm, v_hbm), sources))
         ])
     for load in loads[0]:
@@ -282,9 +282,8 @@
     tap_copy.start()
     for side in sides[1:]:
         side.start()
+    arrived(qkv.at[pl.ds(1, own_heads - 1), :, pl.ds(0, count * rows), :], load_sem.at[3])
     for h in range(1, own_heads):
-        for load in loads[h]:
-            load.wait()
         send_back(h, range(3))
         send_on(h)
 
@@ -415,12 +414,13 @@
             )
 
     def give(h, target, r):
+        group = jnp.where(target // half == upper, 0, jnp.where(seq == inner, 2 + h, 1))
         start = pl.multiple_of(target * block + r * rows, rows)
         pltpu.make_async_remote_copy(
             src_ref=obuf.at[h, pl.ds(start, rows), :],
             dst_ref=att.at[:, block_of(h, me)],
             send_sem=osend_sem,
-            recv_sem=orecv_sem.at[h * count + me],
+            recv_sem=orecv_sem.at[group],
             device_id={"seq": target, "rep": r},
             device_id_type=MESH,
         ).start()
@@ -472,17 +472,24 @@
     latent = lat_ref.shape[0]
     squares = jnp.zeros((rows, HEAD_DIM), jnp.float32)
     projected = jnp.zeros((latent, rows), jnp.float32)
-    for h, step in [
-        (h, half * across + step)
-        for across in (1, 0) for h in range(own_heads) for step in range(half)
-    ]:
+    plan = (
+        [(h, chip, 0) for h in range(own_heads) for chip in (seq, mirror)]
+        + [(h, far + 1 - upper, 1) for h in range(own_heads)]
+        + [(h, far + upper, 2 + h) for h in range(own_heads)]
+    )
+    waited = set()
+    for h, chip, group in plan:
+        if group not in waited:
+            waited.add(group)
+            if group == 0:
+                came = obuf.at[:, pl.ds(0, (half * rep_size - 1) * rows), :]
+            elif group == 1:
+                came = obuf.at[:, pl.ds(0, rep_size * rows), :]
+            else:
+                came = obuf.at[h, pl.ds(0, rep_size * rows), :]
+            arrived(came, orecv_sem.at[group])
         for r in range(rep_size):
-            origin = lax.rem(far + step, seq_size) * rep_size + r
-
-            @pl.when(origin != me)
-            def _():
-                arrived(obuf.at[h, pl.ds(0, rows), :], orecv_sem.at[h * count + origin])
-
+            origin = chip * rep_size + r
             cols = block_of(h, origin)
             combined = (
                 stream_ref[:, cols].astype(jnp.float32) + att[:, cols].astype(jnp.float32)
@@ -584,8 +591,8 @@
             pltpu.VMEM((frames, (reach - 2) * columns, 3 * own), jnp.float32),
             pltpu.SemaphoreType.REGULAR((seq_size - 1,)),
             pltpu.SemaphoreType.REGULAR((head_size - 1,)),
-            dma, dma((own_heads,)), dma, dma((own_heads * count,)), dma, dma,
-            dma((3 * own_heads,)), dma((7,)), dma, dma((6,)), dma((5,)),
+            dma, dma((own_heads,)), dma, dma((2 + own_heads,)), dma, dma,
+            dma((4,)), dma((7,)), dma, dma((6,)), dma((5,)),
         ],
         compiler_params=pltpu.CompilerParams(
             collective_id=0, has_side_effects=True, vmem_limit_bytes=48 << 20

time: 75.6 us -> 75.5 us (level)
  no operation moved by 1% of the time
where the time goes in v4:
time: 75.5 us; the launch traced here: 75.2 us
  Pallas kernels  74.5 us (99%)
    pallas_call x1, Pallas kernels, fused(): pl.pallas_call(functools.partial(fused_kernel, seq_size, rep_size, head_s...  73.6 us

profile of v4, /device:TPU:0, one launch (start us, length us, event | category | flops | bytes accessed | tf_op | source)
XLA Modules:
  0.0 75.2 jit_solution(11349823235756085144)
XLA Ops:
  0.6 73.6 %shard_map.130 = (bf16[128,3072]{1,0:T(8,128)(2,1)S(1)}, f32[64,128]{1,0:T(8,128)S(1)}, f32[256,128]{1,0:T(8,128)S(1)}) custom-call(bf16[128,3072]{1,0:T(8,128)(2,1)} %q_hbm.1, bf16[128,3072]{1,0:T(8,128)(2,1)} %k_hbm.1, bf16[128,3072]{1,0:T(8,128)(2,1)} %v_hbm.1, bf16[128,3072]{1,0:T(8,128)(2,1)} %stream_hbm.1, f32[1,3072]{1,0:T(1,128)} %bitcast.8, ...), custom_call_target="tpu_custom_call" | custom-call | tf_op jit(solution)/shard_map/pallas_call | solution.py:570
  74.2 1.0 %shard_map.131 = (bf16[128,3072]{1,0:T(8,128)(2,1)}, f32[64,128]{1,0:T(8,128)}, f32[256,128]{1,0:T(8,128)}) custom-call(bf16[128,3072]{1,0:T(8,128)(2,1)S(1)} %get-tuple-element.9.hid_in, f32[64,128]{1,0:T(8,128)S(1)} %get-tuple-element.10.lat_in, f32[256,128]{1,0:T(8,128)S(1)} %get-tuple-element.11.dec_in), custom_call_target="tpu_custom_call" | custom-call | tf_op jit(solution)/shard_map/pallas_call | solution.py:606
